TPU v7x, 32 devices: a whole 2x2x4 slice. The times are simulated.
32 devices in a mesh: tx: 4 (over x, core), ty: 4 (over z), src: 2 (over y).
Axes of the slice: x: 2, y: 2, z: 4, core: 2. Of those that a mesh axis runs over, the one named last changes fastest.
Arguments:
- spectrum: bfloat16 [2, 512, 512], P(None, ('tx', 'ty'), 'src'), may hold values from -0.0234375 to 0.0234375
- pupil_mask: int32 [256, 256], replicated, may hold values 0 or 1
- source_shifts: int32 [64, 2], P('src'), may hold values from 0 to 256
- source_weights: int32 [64], P('src'), may hold values from 0 to 8, as said below
Outputs:
- acid_level: float32 [2048, 1024], P(('tx', 'src'), 'ty')
Inputs may be any that keep to these rules, and one draw needn't show every extreme that they name: `source_weights`: the 32 consecutive sources of each group (one index of src) hold at least 4 points with weight above 0; some group has all 32 points on.
All inputs are finite; a program needn't handle non-finite values.
Results may differ from a plain program's by a relative error of at most 0.0017.
Values may be sent and summed in bfloat16 or wider, within the bound.
A program may use at most 64 MiB of HBM per device.

v0:
```python
import functools
import math

import jax
import jax.numpy as jnp
from jax import lax
from jax.experimental import pallas as pl
from jax.experimental.pallas import tpu as pltpu
from jax.sharding import PartitionSpec as P

FRAME = 2048
LANES = 128
COLS = 256
EDGE = 8
PACK = 16
GROUP = 2
UNROLL = 4
MESH = pl.DeviceIdType.MESH

diffusion_rate = 0.2


def wave(turns, period):
    quarter = period // 4
    turn = (turns + quarter // 2) // quarter
    angle = (turns - turn * quarter).astype(jnp.float32) * (2 * math.pi / period)
    square = angle * angle
    sine = angle * (1 + square * (-1 / 6 + square * (1 / 120 + square * (-1 / 5040 + square / 362880))))
    cosine = 1 + square * (-1 / 2 + square * (1 / 24 + square * (-1 / 720 + square / 40320)))
    odd = (turn & 1) == 1
    first, second = jnp.where(odd, sine, cosine), jnp.where(odd, cosine, sine)
    return jnp.where(((turn + 1) & 2) == 2, -first, first), jnp.where((turn & 2) == 2, -second, second)


def iota(shape, dim):
    return lax.broadcasted_iota(jnp.int32, shape, dim)


def dot(a, b):
    return jnp.dot(a, b, preferred_element_type=jnp.float32)


def flip_bits(index, mask):
    bit = 1
    while bit <= mask:
        if mask & bit:
            index = index + bit * (1 - 2 * lax.rem(index // bit, 2))
        bit *= 2
    return index


def others(index, count):
    if count & (count - 1) == 0:
        return [flip_bits(index, d) for d in range(1, count)]
    return [lax.rem(index + d, count) for d in range(1, count)]


def nearest(index, count):
    orders = [sorted((i for i in range(count) if i != at), key=lambda i: (abs(i - at), i)) for at in range(count)]
    return [sum(jnp.where(index == at, orders[at][n], 0) for at in range(count)) for n in range(count - 1)]


def row_table(row_ref, count, block, blocks):
    half = row_ref.shape[0] // (2 * GROUP)
    each = LANES // GROUP
    step = FRAME // (count * blocks)
    sample = iota((half, each), 1)
    x = step * (blocks * sample + block)
    cosine, sine = wave((x * iota((half, each), 0)) & (FRAME - 1), FRAME)
    cosine = jnp.where(sample < count, cosine, 0.0)
    sine = jnp.where(sample < count, sine, 0.0)
    none = jnp.zeros((half, each), jnp.float32)
    for g in range(GROUP):
        for part, (real, imag) in enumerate(((cosine, sine), (-sine, cosine))):
            row = [real if n == g else none for n in range(GROUP)] + [imag if n == g else none for n in range(GROUP)]
            at = (2 * g + part) * half
            row_ref[at : at + half] = jnp.concatenate(row, axis=1).astype(jnp.bfloat16)


def col_table(col_ref, t):
    cols, length = col_ref.shape[0] // 2, col_ref.shape[1]
    chunk = 32

    def fill(n, carry):
        start = pl.multiple_of(n * chunk, chunk)
        y = t * cols + start + iota((chunk, length), 0)
        cosine, sine = wave((y * iota((chunk, length), 1)) & (FRAME - 1), FRAME)
        col_ref[pl.ds(start, chunk)] = cosine.astype(jnp.bfloat16)
        col_ref[pl.ds(cols + start, chunk)] = sine.astype(jnp.bfloat16)
        return carry

    lax.fori_loop(0, cols // chunk, fill, 0)


def blend_table(blend_ref, block, blocks):
    _, tall, samples = blend_ref.shape
    rows = tall - 2 * EDGE
    step = FRAME // samples
    count = samples // blocks
    chunk = PACK

    def fill(n, carry):
        start = pl.multiple_of(n * chunk, chunk)
        x = block * rows - EDGE + start + iota((chunk, samples), 0)
        column = iota((chunk, samples), 1)
        owner = column // count
        gap = x - step * (blocks * (column - owner * count) + owner)
        gap = ((gap + FRAME // 2) & (FRAME - 1)) - FRAME // 2
        cosine, sine = wave(gap, 2 * FRAME)
        place = block * rows - EDGE + start + iota((chunk, 1), 0)
        place = place & (2 * step - 1)
        scale = jnp.zeros((chunk, 1), jnp.float32)
        for n in range(2 * step):
            if n % step:
                scale = jnp.where(place == n, math.sin(math.pi * n / step) / samples, scale)
        scale = jnp.where((owner & 1) == 1, -scale, scale)
        here = gap == 0
        table = jnp.where(here, 1.0, scale * cosine / jnp.where(here, 1.0, sine))
        high = table.astype(jnp.bfloat16)
        blend_ref[0, pl.ds(start, chunk)] = high
        blend_ref[1, pl.ds(start, chunk)] = (table - high.astype(jnp.float32)).astype(jnp.bfloat16)
        return carry

    lax.fori_loop(0, tall // chunk, fill, 0)


def gather_kernel(
    sizes, spec_hbm, shift_ref, weight_ref, pupil_hbm, all_ref, shifts_ref, weights_ref, row_ref, col_ref, mask_ref,
    blend_ref, spec_ref, pupil_ref, local_sem, send_sem, recv_sem, side_send, side_recv,
):
    tx_count, ty_count, src_count = sizes
    pair_count = tx_count // 2
    tx, t, s = lax.axis_index("tx"), lax.axis_index("ty"), lax.axis_index("src")
    pair, core = tx // 2, lax.rem(tx, 2)
    other_core = 1 - core
    far_t = nearest(t, ty_count)
    far_s = others(s, src_count)
    far_pair = others(pair, pair_count)

    def along_ty(i):
        return {"tx": tx, "ty": i, "src": s}

    def along_src(i):
        return {"tx": tx, "ty": t, "src": i}

    def along_pair(i):
        return {"tx": 2 * i + core, "ty": t, "src": s}

    loads = [
        pltpu.make_async_copy(src, dst, local_sem.at[n])
        for n, (src, dst) in enumerate(
            (
                (spec_hbm, spec_ref),
                (pupil_hbm, pupil_ref),
                (shift_ref, shifts_ref.at[s]),
                (weight_ref, weights_ref.at[s]),
            )
        )
    ]
    for load in loads:
        load.start()

    across = {"tx": 2 * pair + other_core, "ty": t, "src": s}
    partners = [along_ty(i) for i in far_t] + [along_src(i) for i in far_s]
    partners += [along_pair(i) for i in far_pair] + [across]
    barrier = pltpu.get_barrier_semaphore()
    for partner in partners:
        pl.semaphore_signal(barrier, inc=1, device_id=partner, device_id_type=MESH)
    pl.semaphore_wait(barrier, len(partners))
    loads[0].wait()

    started = []
    own = (tx, t, s)

    both = slice(None)

    def part(plane, piece):
        i, j, k = piece
        return all_ref.at[k, plane, i, j], recv_sem.at[0 if plane is both else plane, k, i, j]

    def send(plane, piece, device):
        slot, arrived = part(plane, piece)
        copy = pltpu.make_async_remote_copy(
            src_ref=spec_ref if piece is own else slot,
            dst_ref=slot,
            send_sem=send_sem.at[len(started)],
            recv_sem=arrived,
            device_id=device,
            device_id_type=MESH,
        )
        copy.start()
        started.append(copy)

    def arrive(plane, piece):
        slot, arrived = part(plane, piece)
        pltpu.make_async_remote_copy(
            src_ref=slot,
            dst_ref=slot,
            send_sem=send_sem.at[0],
            recv_sem=arrived,
            device_id=across,
            device_id_type=MESH,
        ).wait_recv()

    def spread(piece):
        for i in far_s:
            send(both, piece, along_src(i))
        for i in far_pair:
            send(both, piece, along_pair(i))

    for i in far_t:
        send(both, own, along_ty(i))
    spread(own)
    send(both, own, across)

    side = []
    for n, i in enumerate(far_s):
        for m, (src, dst) in enumerate(((shift_ref, shifts_ref), (weight_ref, weights_ref))):
            copy = pltpu.make_async_remote_copy(
                src_ref=src,
                dst_ref=dst.at[s],
                send_sem=side_send.at[m, n],
                recv_sem=side_recv.at[m, s],
                device_id=along_src(i),
                device_id_type=MESH,
            )
            copy.start()
            side.append(copy)

    for load in loads[1:]:
        load.wait()
    for plane in range(2):
        all_ref[s, plane, tx, t] = spec_ref[plane]
    block = tx * src_count + s
    blocks = tx_count * src_count
    row_table(row_ref, blend_ref.shape[2] // blocks, block, blocks)
    col_table(col_ref, t)
    mask_ref[...] = pupil_ref[...].astype(jnp.float32).T.astype(jnp.bfloat16)

    def second(j):
        for k in far_s:
            arrive(both, (tx, j, k))
            for i in far_pair:
                send(0, (tx, j, k), along_pair(i))
        for i in far_pair:
            there = 2 * i + core
            arrive(both, (there, j, s))
            for k in far_s:
                send(1, (there, j, s), along_src(k))
        if j is not t:
            send(both, (tx, j, s), across)
        for k in far_s:
            send(both, (tx, j, k), across)
        for i in far_pair:
            send(both, (2 * i + core, j, s), across)

    near_first = [t] + far_t
    for n, j in enumerate(far_t):
        arrive(both, (tx, j, s))
        spread((tx, j, s))
        if n == 0:
            second(t)
    blend_table(blend_ref, block, blocks)
    for j in far_t:
        second(j)
    for j in near_first:
        for i in far_pair:
            for k in far_s:
                for plane in range(2):
                    arrive(plane, (2 * i + core, j, k))
                send(both, (2 * i + core, j, k), across)
    for j in near_first:
        for i in [pair] + far_pair:
            for k in [s] + far_s:
                arrive(both, (2 * i + other_core, j, k))
    for n, i in enumerate(far_s):
        for m, (src, dst) in enumerate(((shift_ref, shifts_ref), (weight_ref, weights_ref))):
            pltpu.make_async_remote_copy(
                src_ref=src,
                dst_ref=dst.at[i],
                send_sem=side_send.at[m, n],
                recv_sem=side_recv.at[m, i],
                device_id=across,
                device_id_type=MESH,
            ).wait_recv()
    for copy in started + side:
        copy.wait_send()


def gather(spectrum, source_shifts, source_weights, pupil_mask, sizes, cols):
    tx_count, ty_count, src_count = sizes
    pair_count = tx_count // 2
    _, block_rows, block_cols = spectrum.shape
    slots = source_weights.shape[0]
    length = pupil_mask.shape[0]
    blocks = tx_count * src_count
    samples = 2 * length
    vmem = pl.BlockSpec(memory_space=pltpu.VMEM)
    lines = pair_count * src_count * ty_count
    sends = ty_count - 1 + lines + ty_count * (src_count - 1 + pair_count - 1)
    sends += 2 * ty_count * (src_count - 1) * (pair_count - 1)
    return pl.pallas_call(
        functools.partial(gather_kernel, sizes),
        out_shape=(
            jax.ShapeDtypeStruct((src_count, 2, tx_count, ty_count, block_rows, block_cols), jnp.bfloat16),
            jax.ShapeDtypeStruct((src_count, 2, slots), jnp.int32),
            jax.ShapeDtypeStruct((src_count, 1, slots), jnp.int32),
            jax.ShapeDtypeStruct((GROUP * length, 2 * LANES), jnp.bfloat16),
            jax.ShapeDtypeStruct((2 * cols, length), jnp.bfloat16),
            jax.ShapeDtypeStruct((length, length), jnp.bfloat16),
            jax.ShapeDtypeStruct((2, FRAME // blocks + 2 * EDGE, samples), jnp.bfloat16),
        ),
        in_specs=[pl.BlockSpec(memory_space=pltpu.HBM)] * 4,
        out_specs=(vmem,) * 7,
        scratch_shapes=[
            pltpu.VMEM(spectrum.shape, jnp.bfloat16),
            pltpu.VMEM(pupil_mask.shape, jnp.int32),
            pltpu.SemaphoreType.DMA((4,)),
            pltpu.SemaphoreType.DMA((sends,)),
            pltpu.SemaphoreType.DMA((2, src_count, tx_count, ty_count)),
            pltpu.SemaphoreType.DMA((2, src_count)),
            pltpu.SemaphoreType.DMA((2, src_count)),
        ],
        compiler_params=pltpu.CompilerParams(collective_id=0, has_side_effects=True, vmem_limit_bytes=12 << 20),
        name="gather",
    )(*(pltpu.with_memory_space_constraint(a, pltpu.HBM) for a in (spectrum, source_shifts.T, source_weights[None], pupil_mask)))


def image_kernel(
    sizes, shifts, weights, spec_ref, mask_ref, row_ref, col_ref, out_ref, strip_ref, spec, acc, folded, inner, live
):
    src_count, _, slots = weights.shape
    source_count = src_count * slots
    length = col_ref.shape[1]
    cols = col_ref.shape[0] // 2
    count_x = out_ref.shape[0]
    height, part = spec_ref.shape[2:]
    tiles = height // LANES
    side = 2 * LANES
    block = lax.axis_index("tx") * src_count + lax.axis_index("src")
    power = lax.rem(block, 4)
    flip = 2 * lax.rem(power, 2)
    middle = (lax.rem(4 - power, 4), power + 1 - 2 * lax.rem(power, 2))

    def pick(turn, count):
        for n in range(unroll):
            i = turn * unroll + n
            group, slot = (n // slots, n % slots) if unroll == source_count else (i // slots, lax.rem(i, slots))
            weight = weights[group, 0, slot]
            live[count + GROUP] = shifts[group, 0, slot] + (shifts[group, 1, slot] << 10) + (weight << 20)
            count = count + jnp.minimum(weight, 1)
        return count

    for g in range(GROUP):
        live[g] = 0
    unroll = min(source_count, 64)
    count = jnp.int32(0)
    if unroll == source_count:
        count = pick(0, count)
    else:
        count = lax.fori_loop(0, source_count // unroll, pick, count)
    for g in range((UNROLL + 1) * GROUP):
        live[count + GROUP + g] = 0

    same = jnp.where(iota((side, side), 0) == iota((side, side), 1), 1.0, 0.0).astype(jnp.bfloat16)
    turned = (((1,), (1,)), ((), ()))
    for plane in range(2):
        for i in range(height // side):
            rows = slice(side * i, side * (i + 1))
            for j in range(src_count * part // side):
                cells = [spec_ref[k, plane, rows] for k in range(side * j // part, -(-side * (j + 1) // part))]
                cell = cells[0] if len(cells) == 1 else jnp.concatenate(cells, axis=1)
                value = lax.dot_general(same, cell, turned, preferred_element_type=jnp.float32)
                for n in range(side // LANES):
                    tile = value[:, n * LANES : (n + 1) * LANES]
                    at = side // LANES * i + n
                    spec[plane * tiles + at, side * j : side * (j + 1)] = tile
                    spec[(plane + 2) * tiles + at, side * j : side * (j + 1)] = -tile

    acc[...] = jnp.zeros_like(acc)
    lane = iota((length, LANES), 1)

    def fold(word, slot, at):
        a, b = word & 1023, (word >> 10) & 1023
        tile, rest = a // LANES, lax.rem(a, LANES)
        rows = pl.ds(b, length)
        keep = lane >= rest
        low = pltpu.roll(mask_ref[:, :LANES], rest, 1)
        high = pltpu.roll(mask_ref[:, LANES:], rest, 1)
        ends = jnp.where(keep, low, high)
        centre = jnp.where(keep, high, low)
        last = jnp.minimum(tile + 2, tiles - 1)
        for plane in range(2):
            outer = jnp.where(keep, spec[plane * tiles + tile, rows, :], spec[(plane + flip) * tiles + last, rows, :]).astype(jnp.bfloat16)
            between = spec[middle[plane] * tiles + tile + 1, rows, :].astype(jnp.bfloat16)
            slot[:, at + plane * LANES : at + (plane + 1) * LANES] = outer * ends + between * centre

    first_half = iota((1, LANES), 1) < LANES // 2

    def step(n, parity):
        for g in range(GROUP):
            fold(live[(n + 2) * GROUP + g], folded[1 - parity], 2 * g * LANES)
        inner[parity][...] = dot(folded[parity][...], row_ref[...]).astype(jnp.bfloat16)
        wide = dot(col_ref[...], inner[1 - parity][...])
        real = wide[:cols, :LANES] - wide[cols:, LANES:]
        imag = wide[:cols, LANES:] + wide[cols:, :LANES]
        pair = [(live[n * GROUP + g] >> 20).astype(jnp.float32) for g in range(GROUP)]
        acc[...] += jnp.where(first_half, pair[0], pair[1]) * (real * real + imag * imag)

    inner[1][...] = jnp.zeros_like(inner[1])
    for g in range(GROUP):
        fold(live[GROUP + g], folded[0], 2 * g * LANES)

    def turn_body(turn_index, carry):
        for g in range(UNROLL):
            step(turn_index * UNROLL + g, g % 2)
        return carry

    steps = (count + GROUP - 1) // GROUP + 1
    lax.fori_loop(0, (steps + UNROLL - 1) // UNROLL, turn_body, 0)
    level = acc[...]
    level = (level + pltpu.roll(level, LANES // 2, 1)) / (2.0 * source_count)
    out_ref[...] = level.T[:count_x].astype(jnp.bfloat16)
    strip_ref[0] = level[:PACK, :count_x].astype(jnp.bfloat16)
    strip_ref[1] = level[cols - PACK :, :count_x].astype(jnp.bfloat16)


def image(spectrum, shifts, weights, row_table, col_table, masks, count_x, sizes):
    source_count = weights.shape[0] * weights.shape[2]
    src_count, _, height, part = spectrum.shape
    cols, length = col_table.shape[0] // 2, col_table.shape[1]
    smem = pl.BlockSpec(memory_space=pltpu.SMEM)
    vmem = pl.BlockSpec(memory_space=pltpu.VMEM)
    return pl.pallas_call(
        functools.partial(image_kernel, sizes),
        out_shape=(
            jax.ShapeDtypeStruct((count_x, cols), jnp.bfloat16),
            jax.ShapeDtypeStruct((2, PACK, count_x), jnp.bfloat16),
        ),
        in_specs=[smem, smem, vmem, vmem, vmem, vmem],
        out_specs=(vmem, vmem),
        scratch_shapes=[
            pltpu.VMEM((4 * height // LANES, src_count * part, LANES), jnp.float32),
            pltpu.VMEM((cols, LANES), jnp.float32),
            [pltpu.VMEM((length, GROUP * 2 * LANES), jnp.bfloat16)] * 2,
            [pltpu.VMEM((length, 2 * LANES), jnp.bfloat16)] * 2,
            pltpu.SMEM((source_count + (UNROLL + 3) * GROUP,), jnp.int32),
        ],
        compiler_params=pltpu.CompilerParams(vmem_limit_bytes=16 << 20),
        name="image",
    )(shifts, weights, spectrum, masks, row_table, col_table)


def exchange_kernel(sizes, own_ref, strip_ref, all_ref, beside, send_sem, recv_sem, side_send, side_recv):
    tx_count, ty_count, src_count = sizes
    pair_count = tx_count // 2
    tx, t, s = lax.axis_index("tx"), lax.axis_index("ty"), lax.axis_index("src")
    pair, core = tx // 2, lax.rem(tx, 2)
    far_s = [s] + others(s, src_count)
    far_pair = [pair] + others(pair, pair_count)
    chips = [(i, k) for k in far_s for i in far_pair]

    def device(chip, other, z):
        return {"tx": 2 * chip[0] + (1 - core if other else core), "ty": z, "src": chip[1]}

    def block(chip, other):
        return (2 * chip[0] + (1 - core if other else core)) * src_count + chip[1]

    across = device(chips[0], True, t)
    barrier = pltpu.get_barrier_semaphore()

    def greet(chip, z):
        pl.semaphore_signal(barrier, inc=1, device_id=device(chip, False, z), device_id_type=MESH)

    has = (t > 0, t < ty_count - 1)
    beside[...] = jnp.zeros_like(beside)
    pl.semaphore_signal(barrier, inc=1, device_id=across, device_id_type=MESH)
    for chip in chips[1:]:
        greet(chip, t)
    for side in range(2):

        @pl.when(has[side])
        def _():
            for chip in chips:
                greet(chip, t + 2 * side - 1)

    all_ref[block(chips[0], False)] = own_ref[...]
    sides = jnp.minimum(t, 1) + jnp.minimum(ty_count - 1 - t, 1)
    pl.semaphore_wait(barrier, len(chips) * (1 + sides))

    def copy(src, dst, send, recv, target):
        return pltpu.make_async_remote_copy(
            src_ref=src, dst_ref=dst, send_sem=send, recv_sem=recv, device_id=target, device_id_type=MESH
        )

    def level_copy(n, chip, other, target, own=False):
        at = block(chip, other)
        return copy(own_ref if own else all_ref.at[at], all_ref.at[at], send_sem.at[n], recv_sem.at[at], target)

    def side_copy(n, side, chip, other, target, own=False):
        at = block(chip, other)
        slot = beside.at[side, at]
        return copy(strip_ref.at[1 - side] if own else slot, slot, side_send.at[side, n], side_recv.at[side, at], target)

    started = []
    for n, chip in enumerate(chips[1:]):
        started.append(level_copy(n, chips[0], False, device(chip, False, t), True))
        started[-1].start()
    for side in range(2):

        @pl.when(has[1 - side])
        def _():
            for n, chip in enumerate(chips):
                side_copy(n, side, chips[0], False, device(chip, False, t + 1 - 2 * side), True).start()

    n = len(chips) - 1
    started.append(level_copy(n, chips[0], False, across, True))
    started[-1].start()
    for chip in chips[1:]:
        n += 1
        level_copy(0, chip, False, across).wait_recv()
        started.append(level_copy(n, chip, False, across))
        started[-1].start()
    for side in range(2):

        @pl.when(has[side])
        def _():
            for n, chip in enumerate(chips):
                side_copy(0, side, chip, False, across).wait_recv()
                side_copy(len(chips) + n, side, chip, False, across).start()

    for chip in chips:
        level_copy(0, chip, True, across).wait_recv()
    for side in range(2):

        @pl.when(has[side])
        def _():
            for n, chip in enumerate(chips):
                side_copy(0, side, chip, True, across).wait_recv()
                side_copy(len(chips) + n, side, chip, False, across).wait_send()

        @pl.when(has[1 - side])
        def _():
            for n, chip in enumerate(chips):
                side_copy(n, side, chips[0], False, device(chip, False, t + 1 - 2 * side), True).wait_send()

    for one in started:
        one.wait_send()


def exchange(level, strips, sizes):
    tx_count, ty_count, src_count = sizes
    blocks = tx_count * src_count
    vmem = pl.BlockSpec(memory_space=pltpu.VMEM)
    return pl.pallas_call(
        functools.partial(exchange_kernel, sizes),
        out_shape=(
            jax.ShapeDtypeStruct((blocks,) + level.shape, level.dtype),
            jax.ShapeDtypeStruct((2, blocks) + strips.shape[1:], strips.dtype),
        ),
        in_specs=[vmem] * 2,
        out_specs=(vmem,) * 2,
        scratch_shapes=[
            pltpu.SemaphoreType.DMA((blocks,)),
            pltpu.SemaphoreType.DMA((blocks,)),
            pltpu.SemaphoreType.DMA((2, blocks)),
            pltpu.SemaphoreType.DMA((2, blocks)),
        ],
        compiler_params=pltpu.CompilerParams(collective_id=1, has_side_effects=True, vmem_limit_bytes=4 << 20),
        name="exchange",
    )(level, strips)


def diffuse_kernel(sizes, all_ref, beside, blend_ref, out_ref):
    tx_count, ty_count, src_count = sizes
    rows, cols = out_ref.shape
    blocks, count, _ = all_ref.shape
    samples = blocks * count
    tall = rows + 2 * EDGE
    level = all_ref[...].reshape(samples, cols)
    sides = [jnp.concatenate([beside[side, n] for n in range(blocks)], axis=1) for side in range(2)]
    strip = jnp.concatenate([sides[1], jnp.zeros((LANES - 2 * PACK, samples), jnp.bfloat16), sides[0]], axis=0)
    turned = (((1,), (1,)), ((), ()))
    middle = dot(blend_ref[0], level) + dot(blend_ref[1], level)
    edge = lax.dot_general(blend_ref[0], strip, turned, preferred_element_type=jnp.float32)
    edge += lax.dot_general(blend_ref[1], strip, turned, preferred_element_type=jnp.float32)
    acid = 1.0 - jnp.exp(-jnp.concatenate([middle, edge], axis=1))
    wide = cols + LANES
    row_block = lax.axis_index("tx") * src_count + lax.axis_index("src")
    col_block = lax.axis_index("ty")
    x = row_block * rows - EDGE + iota(acid.shape, 0)
    column = iota(acid.shape, 1)
    y = col_block * cols + jnp.where(column >= cols + LANES // 2, column - wide, column)
    inside = (x >= 0) & (x < blocks * rows) & (y >= 0) & (y < ty_count * cols)
    for repeat in range(2):
        acid = jnp.where(inside, acid, 0.0)
        near = (
            pltpu.roll(acid, 1, 0)
            + pltpu.roll(acid, tall - 1, 0)
            + pltpu.roll(acid, 1, 1)
            + pltpu.roll(acid, wide - 1, 1)
        )
        acid = acid + diffusion_rate * (near - 4.0 * acid)
    out_ref[...] = acid[EDGE : EDGE + rows, :cols]


def diffuse(levels, beside, blend, sizes):
    rows = blend.shape[1] - 2 * EDGE
    vmem = pl.BlockSpec(memory_space=pltpu.VMEM)
    return pl.pallas_call(
        functools.partial(diffuse_kernel, sizes),
        out_shape=jax.ShapeDtypeStruct((rows, levels.shape[2]), jnp.float32),
        in_specs=[vmem] * 3,
        out_specs=vmem,
        compiler_params=pltpu.CompilerParams(vmem_limit_bytes=12 << 20),
        name="diffuse",
    )(levels, beside, blend)


def body(sizes, cols, spectrum, pupil_mask, source_shifts, source_weights):
    pieces, shifts, weights, row_table, col_table, masks, blend = gather(
        spectrum, source_shifts, source_weights, pupil_mask, sizes, cols
    )
    src_count, _, tx_count, ty_count, block_rows, block_cols = pieces.shape
    columns = pieces.reshape(src_count, 2, tx_count * ty_count * block_rows, block_cols)
    count_x = blend.shape[2] // (tx_count * src_count)
    level, strips = image(columns, shifts, weights, row_table, col_table, masks, count_x, sizes)
    levels, beside = exchange(level, strips, sizes)
    return diffuse(levels, beside, blend, sizes)


def solution(mesh):
    sizes = (mesh.shape["tx"], mesh.shape["ty"], mesh.shape["src"])
    placed = (P(None, ("tx", "ty"), "src"), P(), P("src", None), P("src"))
    return jax.shard_map(
        functools.partial(body, sizes, COLS),
        mesh=mesh,
        in_specs=placed,
        out_specs=P(("tx", "src"), "ty"),
        check_vma=False,
    )
```

profile of v0, /device:TPU:0, one launch (start us, length us, event | category | flops | bytes accessed | tf_op | source)
XLA Modules:
  0.0 34.5 jit_solution(3691536472502992733)
XLA Ops:
  0.0 18.0 %gather.1 = (bf16[2,2,4,4,32,256]{5,4,3,2,1,0:T(8,128)(2,1)S(1)}, s32[2,2,32]{2,1,0:T(2,128)S(1)}, s32[2,1,32]{2,1,0:T(1,128)S(1)}, bf16[512,256]{1,0:T(8,128)(2...) custom-call(bf16[2,32,256]{2,1,0:T(8,128)(2,1)} %spec_hbm.1, ...), custom_call_target="tpu_custom_call" | custom-call | tf_op jit(solution)/shard_map/gather/pallas_call | solution.py:302
  18.0 7.7 %image.1 = (bf16[64,256]{1,0:T(8,128)(2,1)S(1)}, bf16[2,16,64]{2,1,0:T(8,128)(2,1)S(1)}) custom-call(s32[2,2,32]{2,1,0:T(2,128)S(1)} %get-tuple-element.16.shifts, s32[2,1,32]{2,1,0:T(1,128)S(1)} %get-tuple-element.17.weights, bf16[2,2,512,256]{3,2,1,0:T(8,128)(2,1)S(1)} %bitcast.3, bf16[256,256]{1,0:T(8,128)(2,1)S(1)} %get-tuple-element.19.mask_ref, ...), custom_call_target="tpu_custom_call" | custom-call | tf_op jit(solution)/shard_map/image/pallas_call | solution.py:434
  25.7 7.2 %exchange.1 = (bf16[8,64,256]{2,1,0:T(8,128)(2,1)S(1)}, bf16[2,8,16,64]{3,2,1,0:T(8,128)(2,1)S(1)}) custom-call(bf16[64,256]{1,0:T(8,128)(2,1)S(1)} %get-tuple-element.22.own_ref, bf16[2,16,64]{2,1,0:T(8,128)(2,1)S(1)} %get-tuple-element.23.strip_ref), custom_call_target="tpu_custom_call" | custom-call | tf_op jit(solution)/shard_map/exchange/pallas_call | solution.py:555
  32.9 1.6 %diffuse.1 = f32[256,256]{1,0:T(8,128)} custom-call(bf16[8,64,256]{2,1,0:T(8,128)(2,1)S(1)} %get-tuple-element.24.all_ref, bf16[2,8,16,64]{3,2,1,0:T(8,128)(2,1)S(1)} %get-tuple-element.25.beside, bf16[2,272,512]{2,1,0:T(8,128)(2,1)S(1)} %get-tuple-element.26.blend_ref), custom_call_target="tpu_custom_call" | custom-call | tf_op jit(solution)/shard_map/diffuse/pallas_call | solution.py:610
where the time goes:
time: 35.2 us; the launch traced here: 34.5 us
  Pallas kernels  34.5 us (98%)
    pallas_call x1, Pallas kernels, gather(): pl.pallas_call(functools.partial(gather_kernel, sizes), out_shape=(jax.Sh...  18 us
    pallas_call x1, Pallas kernels, image(): pl.pallas_call(functools.partial(image_kernel, sizes), out_shape=(jax.Sha...  7.71 us
    pallas_call x1, Pallas kernels, exchange(): pl.pallas_call(functools.partial(exchange_kernel, sizes), out_shape=(jax....  7.18 us
    pallas_call x1, Pallas kernels, diffuse(): pl.pallas_call(functools.partial(diffuse_kernel, sizes), out_shape=jax.Sh...  1.64 us

commit v1 on v0

--- a/solution.py
+++ b/solution.py
@@ -15,6 +15,7 @@
 PACK = 16
 GROUP = 2
 UNROLL = 4
+TAIL = 4
 MESH = pl.DeviceIdType.MESH
 
 diffusion_rate = 0.2
@@ -125,8 +126,8 @@
 
 
 def gather_kernel(
-    sizes, spec_hbm, shift_ref, weight_ref, pupil_hbm, all_ref, shifts_ref, weights_ref, row_ref, col_ref, mask_ref,
-    blend_ref, spec_ref, pupil_ref, local_sem, send_sem, recv_sem, side_send, side_recv,
+    sizes, spec_hbm, shift_ref, weight_ref, pupil_hbm, turned_ref, word_ref, row_ref, col_ref, mask_ref, blend_ref,
+    shifts_ref, weights_ref, all_ref, spec_ref, pupil_ref, local_sem, send_sem, recv_sem, side_send, side_recv,
 ):
     tx_count, ty_count, src_count = sizes
     pair_count = tx_count // 2
@@ -236,6 +237,17 @@
     row_table(row_ref, blend_ref.shape[2] // blocks, block, blocks)
     col_table(col_ref, t)
     mask_ref[...] = pupil_ref[...].astype(jnp.float32).T.astype(jnp.bfloat16)
+
+    part_rows, part_cols = ty_count * spec_ref.shape[1], spec_ref.shape[2]
+    same = jnp.where(iota((part_cols,) * 2, 0) == iota((part_cols,) * 2, 1), 1.0, 0.0).astype(jnp.bfloat16)
+
+    def turn(i, k):
+        rows = pl.ds(pl.multiple_of(k * part_cols, part_cols), part_cols)
+        for plane in range(2):
+            cell = all_ref[k, plane, i].reshape(part_rows, part_cols)
+            value = lax.dot_general(same, cell, (((1,), (1,)), ((), ())), preferred_element_type=jnp.float32)
+            turned_ref[plane * tx_count + i, rows] = value
+            turned_ref[(plane + 2) * tx_count + i, rows] = -value
 
     def second(j):
         for k in far_s:
@@ -260,19 +272,23 @@
         spread((tx, j, s))
         if n == 0:
             second(t)
+    turn(tx, s)
     blend_table(blend_ref, block, blocks)
     for j in far_t:
         second(j)
+    for k in far_s:
+        turn(tx, k)
+    for i in far_pair:
+        turn(2 * i + core, s)
     for j in near_first:
         for i in far_pair:
             for k in far_s:
                 for plane in range(2):
                     arrive(plane, (2 * i + core, j, k))
                 send(both, (2 * i + core, j, k), across)
-    for j in near_first:
-        for i in [pair] + far_pair:
-            for k in [s] + far_s:
-                arrive(both, (2 * i + other_core, j, k))
+    for i in far_pair:
+        for k in far_s:
+            turn(2 * i + core, k)
     for n, i in enumerate(far_s):
         for m, (src, dst) in enumerate(((shift_ref, shifts_ref), (weight_ref, weights_ref))):
             pltpu.make_async_remote_copy(
@@ -283,6 +299,12 @@
                 device_id=across,
                 device_id_type=MESH,
             ).wait_recv()
+    word_ref[...] = shifts_ref[:, 0:1] + shifts_ref[:, 1:2] * 1024 + weights_ref[...] * (1 << 20)
+    for i in [pair] + far_pair:
+        for k in [s] + far_s:
+            for j in near_first:
+                arrive(both, (2 * i + other_core, j, k))
+            turn(2 * i + other_core, k)
     for copy in started + side:
         copy.wait_send()
 
@@ -302,8 +324,7 @@
     return pl.pallas_call(
         functools.partial(gather_kernel, sizes),
         out_shape=(
-            jax.ShapeDtypeStruct((src_count, 2, tx_count, ty_count, block_rows, block_cols), jnp.bfloat16),
-            jax.ShapeDtypeStruct((src_count, 2, slots), jnp.int32),
+            jax.ShapeDtypeStruct((4 * tx_count, src_count * block_cols, ty_count * block_rows), jnp.float32),
             jax.ShapeDtypeStruct((src_count, 1, slots), jnp.int32),
             jax.ShapeDtypeStruct((GROUP * length, 2 * LANES), jnp.bfloat16),
             jax.ShapeDtypeStruct((2 * cols, length), jnp.bfloat16),
@@ -311,8 +332,11 @@
             jax.ShapeDtypeStruct((2, FRAME // blocks + 2 * EDGE, samples), jnp.bfloat16),
         ),
         in_specs=[pl.BlockSpec(memory_space=pltpu.HBM)] * 4,
-        out_specs=(vmem,) * 7,
+        out_specs=(vmem,) * 6,
         scratch_shapes=[
+            pltpu.VMEM((src_count, 2, slots), jnp.int32),
+            pltpu.VMEM((src_count, 1, slots), jnp.int32),
+            pltpu.VMEM((src_count, 2, tx_count, ty_count, block_rows, block_cols), jnp.bfloat16),
             pltpu.VMEM(spectrum.shape, jnp.bfloat16),
             pltpu.VMEM(pupil_mask.shape, jnp.int32),
             pltpu.SemaphoreType.DMA((4,)),
@@ -321,34 +345,66 @@
             pltpu.SemaphoreType.DMA((2, src_count)),
             pltpu.SemaphoreType.DMA((2, src_count)),
         ],
-        compiler_params=pltpu.CompilerParams(collective_id=0, has_side_effects=True, vmem_limit_bytes=12 << 20),
+        compiler_params=pltpu.CompilerParams(collective_id=0, has_side_effects=True, vmem_limit_bytes=16 << 20),
         name="gather",
     )(*(pltpu.with_memory_space_constraint(a, pltpu.HBM) for a in (spectrum, source_shifts.T, source_weights[None], pupil_mask)))
 
 
-def image_kernel(
-    sizes, shifts, weights, spec_ref, mask_ref, row_ref, col_ref, out_ref, strip_ref, spec, acc, folded, inner, live
-):
-    src_count, _, slots = weights.shape
-    source_count = src_count * slots
+def stages(sizes, spec, mask_ref, row_ref, col_ref, live):
     length = col_ref.shape[1]
     cols = col_ref.shape[0] // 2
-    count_x = out_ref.shape[0]
-    height, part = spec_ref.shape[2:]
-    tiles = height // LANES
-    side = 2 * LANES
-    block = lax.axis_index("tx") * src_count + lax.axis_index("src")
+    tiles = spec.shape[0] // 4
+    block = lax.axis_index("tx") * sizes[2] + lax.axis_index("src")
     power = lax.rem(block, 4)
     flip = 2 * lax.rem(power, 2)
     middle = (lax.rem(4 - power, 4), power + 1 - 2 * lax.rem(power, 2))
+    lane = iota((length, LANES), 1)
+    first_half = iota((1, LANES), 1) < LANES // 2
+
+    def fold(n, slot):
+        for g in range(GROUP):
+            word = live[(n + 1) * GROUP + g]
+            a, b = word & 1023, (word >> 10) & 1023
+            tile, rest = a // LANES, lax.rem(a, LANES)
+            rows = pl.ds(b, length)
+            keep = lane >= rest
+            low = pltpu.roll(mask_ref[:, :LANES], rest, 1)
+            high = pltpu.roll(mask_ref[:, LANES:], rest, 1)
+            ends = jnp.where(keep, low, high)
+            centre = jnp.where(keep, high, low)
+            last = jnp.minimum(tile + 2, tiles - 1)
+            for plane in range(2):
+                outer = jnp.where(keep, spec[plane * tiles + tile, rows, :], spec[(plane + flip) * tiles + last, rows, :])
+                between = spec[middle[plane] * tiles + tile + 1, rows, :]
+                at = (2 * g + plane) * LANES
+                slot[:, at : at + LANES] = outer.astype(jnp.bfloat16) * ends + between.astype(jnp.bfloat16) * centre
+
+    def cross(source, slot):
+        slot[...] = dot(source[...], row_ref[...]).astype(jnp.bfloat16)
+
+    def square(n, source):
+        wide = dot(col_ref[...], source[...])
+        real = wide[:cols, :LANES] - wide[cols:, LANES:]
+        imag = wide[:cols, LANES:] + wide[cols:, :LANES]
+        pair = [(live[(n + 1) * GROUP + g] >> 20).astype(jnp.float32) for g in range(GROUP)]
+        return jnp.where(first_half, pair[0], pair[1]) * (real * real + imag * imag)
+
+    return fold, cross, square
+
+
+def image_kernel(
+    sizes, words, spec, mask_ref, row_ref, col_ref, live, acc, next_folded, next_inner, other_folded, other_inner
+):
+    src_count, _, slots = words.shape
+    source_count = src_count * slots
 
     def pick(turn, count):
         for n in range(unroll):
             i = turn * unroll + n
             group, slot = (n // slots, n % slots) if unroll == source_count else (i // slots, lax.rem(i, slots))
-            weight = weights[group, 0, slot]
-            live[count + GROUP] = shifts[group, 0, slot] + (shifts[group, 1, slot] << 10) + (weight << 20)
-            count = count + jnp.minimum(weight, 1)
+            word = words[group, 0, slot]
+            live[count + GROUP] = word
+            count = count + jnp.minimum(word >> 20, 1)
         return count
 
     for g in range(GROUP):
@@ -359,99 +415,58 @@
         count = pick(0, count)
     else:
         count = lax.fori_loop(0, source_count // unroll, pick, count)
-    for g in range((UNROLL + 1) * GROUP):
+    for g in range((UNROLL + TAIL) * GROUP):
         live[count + GROUP + g] = 0
 
-    same = jnp.where(iota((side, side), 0) == iota((side, side), 1), 1.0, 0.0).astype(jnp.bfloat16)
-    turned = (((1,), (1,)), ((), ()))
-    for plane in range(2):
-        for i in range(height // side):
-            rows = slice(side * i, side * (i + 1))
-            for j in range(src_count * part // side):
-                cells = [spec_ref[k, plane, rows] for k in range(side * j // part, -(-side * (j + 1) // part))]
-                cell = cells[0] if len(cells) == 1 else jnp.concatenate(cells, axis=1)
-                value = lax.dot_general(same, cell, turned, preferred_element_type=jnp.float32)
-                for n in range(side // LANES):
-                    tile = value[:, n * LANES : (n + 1) * LANES]
-                    at = side // LANES * i + n
-                    spec[plane * tiles + at, side * j : side * (j + 1)] = tile
-                    spec[(plane + 2) * tiles + at, side * j : side * (j + 1)] = -tile
-
+    fold, cross, square = stages(sizes, spec, mask_ref, row_ref, col_ref, live)
+    folded = (next_folded, other_folded)
+    inner = (other_inner, next_inner)
     acc[...] = jnp.zeros_like(acc)
-    lane = iota((length, LANES), 1)
-
-    def fold(word, slot, at):
-        a, b = word & 1023, (word >> 10) & 1023
-        tile, rest = a // LANES, lax.rem(a, LANES)
-        rows = pl.ds(b, length)
-        keep = lane >= rest
-        low = pltpu.roll(mask_ref[:, :LANES], rest, 1)
-        high = pltpu.roll(mask_ref[:, LANES:], rest, 1)
-        ends = jnp.where(keep, low, high)
-        centre = jnp.where(keep, high, low)
-        last = jnp.minimum(tile + 2, tiles - 1)
-        for plane in range(2):
-            outer = jnp.where(keep, spec[plane * tiles + tile, rows, :], spec[(plane + flip) * tiles + last, rows, :]).astype(jnp.bfloat16)
-            between = spec[middle[plane] * tiles + tile + 1, rows, :].astype(jnp.bfloat16)
-            slot[:, at + plane * LANES : at + (plane + 1) * LANES] = outer * ends + between * centre
-
-    first_half = iota((1, LANES), 1) < LANES // 2
-
-    def step(n, parity):
-        for g in range(GROUP):
-            fold(live[(n + 2) * GROUP + g], folded[1 - parity], 2 * g * LANES)
-        inner[parity][...] = dot(folded[parity][...], row_ref[...]).astype(jnp.bfloat16)
-        wide = dot(col_ref[...], inner[1 - parity][...])
-        real = wide[:cols, :LANES] - wide[cols:, LANES:]
-        imag = wide[:cols, LANES:] + wide[cols:, :LANES]
-        pair = [(live[n * GROUP + g] >> 20).astype(jnp.float32) for g in range(GROUP)]
-        acc[...] += jnp.where(first_half, pair[0], pair[1]) * (real * real + imag * imag)
-
-    inner[1][...] = jnp.zeros_like(inner[1])
-    for g in range(GROUP):
-        fold(live[GROUP + g], folded[0], 2 * g * LANES)
+    next_inner[...] = jnp.zeros_like(next_inner)
+    fold(0, folded[0])
 
     def turn_body(turn_index, carry):
         for g in range(UNROLL):
-            step(turn_index * UNROLL + g, g % 2)
+            n = turn_index * UNROLL + g
+            fold(n + 1, folded[1 - g % 2])
+            cross(folded[g % 2], inner[g % 2])
+            acc[...] += square(n - 1, inner[1 - g % 2])
         return carry
 
-    steps = (count + GROUP - 1) // GROUP + 1
-    lax.fori_loop(0, (steps + UNROLL - 1) // UNROLL, turn_body, 0)
-    level = acc[...]
-    level = (level + pltpu.roll(level, LANES // 2, 1)) / (2.0 * source_count)
-    out_ref[...] = level.T[:count_x].astype(jnp.bfloat16)
-    strip_ref[0] = level[:PACK, :count_x].astype(jnp.bfloat16)
-    strip_ref[1] = level[cols - PACK :, :count_x].astype(jnp.bfloat16)
-
-
-def image(spectrum, shifts, weights, row_table, col_table, masks, count_x, sizes):
-    source_count = weights.shape[0] * weights.shape[2]
-    src_count, _, height, part = spectrum.shape
+    steps = (count + GROUP - 1) // GROUP + 1 - TAIL
+    turns = jnp.maximum(steps + UNROLL - 1, 0) // UNROLL
+    live[live.shape[0] - 1] = turns * UNROLL
+    lax.fori_loop(0, turns, turn_body, 0)
+
+
+def image(spectrum, words, row_table, col_table, masks, sizes):
+    source_count = words.shape[0] * words.shape[2]
     cols, length = col_table.shape[0] // 2, col_table.shape[1]
     smem = pl.BlockSpec(memory_space=pltpu.SMEM)
     vmem = pl.BlockSpec(memory_space=pltpu.VMEM)
     return pl.pallas_call(
         functools.partial(image_kernel, sizes),
         out_shape=(
-            jax.ShapeDtypeStruct((count_x, cols), jnp.bfloat16),
-            jax.ShapeDtypeStruct((2, PACK, count_x), jnp.bfloat16),
+            jax.ShapeDtypeStruct((source_count + (UNROLL + TAIL + 2) * GROUP,), jnp.int32),
+            jax.ShapeDtypeStruct((cols, LANES), jnp.float32),
+            jax.ShapeDtypeStruct((length, GROUP * 2 * LANES), jnp.bfloat16),
+            jax.ShapeDtypeStruct((length, 2 * LANES), jnp.bfloat16),
         ),
-        in_specs=[smem, smem, vmem, vmem, vmem, vmem],
-        out_specs=(vmem, vmem),
+        in_specs=[smem, vmem, vmem, vmem, vmem],
+        out_specs=(smem, vmem, vmem, vmem),
         scratch_shapes=[
-            pltpu.VMEM((4 * height // LANES, src_count * part, LANES), jnp.float32),
-            pltpu.VMEM((cols, LANES), jnp.float32),
-            [pltpu.VMEM((length, GROUP * 2 * LANES), jnp.bfloat16)] * 2,
-            [pltpu.VMEM((length, 2 * LANES), jnp.bfloat16)] * 2,
-            pltpu.SMEM((source_count + (UNROLL + 3) * GROUP,), jnp.int32),
+            pltpu.VMEM((length, GROUP * 2 * LANES), jnp.bfloat16),
+            pltpu.VMEM((length, 2 * LANES), jnp.bfloat16),
         ],
-        compiler_params=pltpu.CompilerParams(vmem_limit_bytes=16 << 20),
+        compiler_params=pltpu.CompilerParams(vmem_limit_bytes=12 << 20),
         name="image",
-    )(shifts, weights, spectrum, masks, row_table, col_table)
-
-
-def exchange_kernel(sizes, own_ref, strip_ref, all_ref, beside, send_sem, recv_sem, side_send, side_recv):
+    )(words, spectrum, masks, row_table, col_table)
+
+
+def exchange_kernel(
+    sizes, live_ref, acc, first_folded, first_inner, spec, mask_ref, row_ref, col_ref, all_ref, beside,
+    live, own_ref, strip_ref, folded, inner, live_sem, send_sem, recv_sem, side_send, side_recv,
+):
     tx_count, ty_count, src_count = sizes
     pair_count = tx_count // 2
     tx, t, s = lax.axis_index("tx"), lax.axis_index("ty"), lax.axis_index("src")
@@ -472,6 +487,8 @@
     def greet(chip, z):
         pl.semaphore_signal(barrier, inc=1, device_id=device(chip, False, z), device_id_type=MESH)
 
+    load = pltpu.make_async_copy(live_ref, live, live_sem)
+    load.start()
     has = (t > 0, t < ty_count - 1)
     beside[...] = jnp.zeros_like(beside)
     pl.semaphore_signal(barrier, inc=1, device_id=across, device_id_type=MESH)
@@ -484,7 +501,27 @@
             for chip in chips:
                 greet(chip, t + 2 * side - 1)
 
-    all_ref[block(chips[0], False)] = own_ref[...]
+    fold, cross, square = stages(sizes, spec, mask_ref, row_ref, col_ref, live)
+    load.wait()
+    n = live[live.shape[0] - 1]
+    level = acc[...]
+    source_folded, source_inner = first_folded, first_inner
+    for g in range(TAIL):
+        if g < TAIL - 2:
+            fold(n + g + 1, folded[g % 2])
+        if g < TAIL - 1:
+            cross(source_folded, inner[g % 2])
+        level += square(n + g - 1, source_inner)
+        source_folded, source_inner = folded[g % 2], inner[g % 2]
+
+    cols = level.shape[0]
+    count_x = own_ref.shape[0]
+    level = (level + pltpu.roll(level, LANES // 2, 1)) / (2.0 * (live.shape[0] - (UNROLL + TAIL + 2) * GROUP))
+    own = level.T[:count_x].astype(jnp.bfloat16)
+    own_ref[...] = own
+    strip_ref[0] = level[:PACK, :count_x].astype(jnp.bfloat16)
+    strip_ref[1] = level[cols - PACK :, :count_x].astype(jnp.bfloat16)
+    all_ref[block(chips[0], False)] = own
     sides = jnp.minimum(t, 1) + jnp.minimum(ty_count - 1 - t, 1)
     pl.semaphore_wait(barrier, len(chips) * (1 + sides))
 
@@ -548,27 +585,34 @@
         one.wait_send()
 
 
-def exchange(level, strips, sizes):
+def exchange(live, acc, folded, inner, spectrum, masks, row_table, col_table, count_x, sizes):
     tx_count, ty_count, src_count = sizes
     blocks = tx_count * src_count
     vmem = pl.BlockSpec(memory_space=pltpu.VMEM)
+    cols = acc.shape[0]
     return pl.pallas_call(
         functools.partial(exchange_kernel, sizes),
         out_shape=(
-            jax.ShapeDtypeStruct((blocks,) + level.shape, level.dtype),
-            jax.ShapeDtypeStruct((2, blocks) + strips.shape[1:], strips.dtype),
+            jax.ShapeDtypeStruct((blocks, count_x, cols), jnp.bfloat16),
+            jax.ShapeDtypeStruct((2, blocks, PACK, count_x), jnp.bfloat16),
         ),
-        in_specs=[vmem] * 2,
+        in_specs=[vmem] * 8,
         out_specs=(vmem,) * 2,
         scratch_shapes=[
+            pltpu.SMEM(live.shape, jnp.int32),
+            pltpu.VMEM((count_x, cols), jnp.bfloat16),
+            pltpu.VMEM((2, PACK, count_x), jnp.bfloat16),
+            [pltpu.VMEM(folded.shape, jnp.bfloat16)] * 2,
+            [pltpu.VMEM(inner.shape, jnp.bfloat16)] * 2,
+            pltpu.SemaphoreType.DMA(()),
             pltpu.SemaphoreType.DMA((blocks,)),
             pltpu.SemaphoreType.DMA((blocks,)),
             pltpu.SemaphoreType.DMA((2, blocks)),
             pltpu.SemaphoreType.DMA((2, blocks)),
         ],
-        compiler_params=pltpu.CompilerParams(collective_id=1, has_side_effects=True, vmem_limit_bytes=4 << 20),
+        compiler_params=pltpu.CompilerParams(collective_id=1, has_side_effects=True, vmem_limit_bytes=12 << 20),
         name="exchange",
-    )(level, strips)
+    )(live, acc, folded, inner, spectrum, masks, row_table, col_table)
 
 
 def diffuse_kernel(sizes, all_ref, beside, blend_ref, out_ref):
@@ -618,14 +662,12 @@
 
 
 def body(sizes, cols, spectrum, pupil_mask, source_shifts, source_weights):
-    pieces, shifts, weights, row_table, col_table, masks, blend = gather(
+    turned, words, row_table, col_table, masks, blend = gather(
         spectrum, source_shifts, source_weights, pupil_mask, sizes, cols
     )
-    src_count, _, tx_count, ty_count, block_rows, block_cols = pieces.shape
-    columns = pieces.reshape(src_count, 2, tx_count * ty_count * block_rows, block_cols)
-    count_x = blend.shape[2] // (tx_count * src_count)
-    level, strips = image(columns, shifts, weights, row_table, col_table, masks, count_x, sizes)
-    levels, beside = exchange(level, strips, sizes)
+    count_x = blend.shape[2] // (sizes[0] * sizes[2])
+    live, acc, folded, inner = image(turned, words, row_table, col_table, masks, sizes)
+    levels, beside = exchange(live, acc, folded, inner, turned, masks, row_table, col_table, count_x, sizes)
     return diffuse(levels, beside, blend, sizes)
 
 

time: 35.2 us -> 34.2 us (0.972); the launches traced: 34.5 us -> 34 us
  Pallas kernels: 34.5 us -> 34 us
    pallas_call x1, Pallas kernels: 7.71 us -> 6.75 us  [image(): pl.pallas_call(functools.partial(image_kernel, sizes), out_shape=(jax.Sha...]
    pallas_call x1, Pallas kernels: 18 us -> 18.6 us  [gather(): pl.pallas_call(functools.partial(gather_kernel, sizes), out_shape=(jax.Sh...]
where the time goes in v1:
time: 34.2 us; the launch traced here: 34 us
  Pallas kernels  34 us (99%)
    pallas_call x1, Pallas kernels, gather(): pl.pallas_call(functools.partial(gather_kernel, sizes), out_shape=(jax.Sh...  18.6 us
    pallas_call x1, Pallas kernels, exchange(): pl.pallas_call(functools.partial(exchange_kernel, sizes), out_shape=(jax....  7.04 us
    pallas_call x1, Pallas kernels, image(): pl.pallas_call(functools.partial(image_kernel, sizes), out_shape=(jax.Sha...  6.75 us
    pallas_call x1, Pallas kernels, diffuse(): pl.pallas_call(functools.partial(diffuse_kernel, sizes), out_shape=jax.Sh...  1.64 us

profile of v1, /device:TPU:0, one launch (start us, length us, event | category | flops | bytes accessed | tf_op | source)
XLA Modules:
  0.0 34.0 jit_solution(13231838465731176708)
XLA Ops:
  0.0 18.6 %gather.1 = (f32[16,512,128]{2,1,0:T(8,128)S(1)}, s32[2,1,32]{2,1,0:T(1,128)S(1)}, bf16[512,256]{1,0:T(8,128)(2,1)S(1)}, bf16[512,256]{1,0:T(8,128)(2,1)S(1)}, b...) custom-call(bf16[2,32,256]{2,1,0:T(8,128)(2,1)} %spec_hbm.1, s32[2,32]{1,0:T(2,128)} %bitcast.2, ...), custom_call_target="tpu_custom_call" | custom-call | tf_op jit(solution)/shard_map/gather/pallas_call | solution.py:324
  18.6 6.8 %image.1 = (s32[84]{0:T(128)S(1)}, f32[256,128]{1,0:T(8,128)S(1)}, bf16[256,512]{1,0:T(8,128)(2,1)S(1)}, bf16[256,256]{1,0:T(8,128)(2,1)S(1)}) custom-call(s32[2,1,32]{2,1,0:T(1,128)S(1)} %get-tuple-element.17.words, f32[16,512,128]{2,1,0:T(8,128)S(1)} %get-tuple-element.18.spec, bf16[256,256]{1,0:T(8,128)(2,1)S(1)} %get-tuple-element.19.mask_ref, ...), custom_call_target="tpu_custom_call" | custom-call | tf_op jit(solution)/shard_map/image/pallas_call | solution.py:447
  25.4 7.0 %exchange.1 = (bf16[8,64,256]{2,1,0:T(8,128)(2,1)S(1)}, bf16[2,8,16,64]{3,2,1,0:T(8,128)(2,1)S(1)}) custom-call(s32[84]{0:T(128)S(1)} %get-tuple-element.22.live_ref, f32[256,128]{1,0:T(8,128)S(1)} %get-tuple-element.23.acc, bf16[256,512]{1,0:T(8,128)(2,1)S(1)} %get-tuple-element.24.first_folded, bf16[256,256]{1,0:T(8,128)(2,1)S(1)} %get-tuple-element.25.first_inner, ...), custom_call_target="tpu_custom_call" | custom-call | tf_op jit(solution)/shard_map/exchange/pallas_call | solution.py:593
  32.4 1.6 %diffuse.1 = f32[256,256]{1,0:T(8,128)} custom-call(bf16[8,64,256]{2,1,0:T(8,128)(2,1)S(1)} %get-tuple-element.26.all_ref, bf16[2,8,16,64]{3,2,1,0:T(8,128)(2,1)S(1)} %get-tuple-element.27.beside, bf16[2,272,512]{2,1,0:T(8,128)(2,1)S(1)} %get-tuple-element.28.blend_ref), custom_call_target="tpu_custom_call" | custom-call | tf_op jit(solution)/shard_map/diffuse/pallas_call | solution.py:654
